TPU v7x, 32 devices: a whole 2x2x4 slice. The times are simulated.
32 devices in a mesh: front: 2 (over core), row: 4 (over y, x), col: 4 (over z).
Axes of the slice: x: 2, y: 2, z: 4, core: 2. Of those that a mesh axis runs over, the one named last changes fastest.
Arguments:
- front_rows: float32 [4096, 24576], P(('front', 'row'), 'col'), parts along dimension 0, may hold values from -0.0546875 to 0.0546875
- random_columns: bfloat16 [49152, 512], P(('front', 'col'), 'row'), parts along dimension 0, may hold values from -6 to 6
Outputs:
- basis: float32 [4096, 256], P(('front', 'row', 'col')), parts along dimension 0
- projected: float32 [1024, 512], P(('front', 'row')), parts along dimension 0
There are 2 independent parts, one for each index of `front`. A program takes and returns all parts, laid end to end along the dimension named above; each array names one. Nothing has to cross between parts.
All inputs are finite; a program needn't handle non-finite values.
Results may differ from a plain program's by a relative error of at most 0.0003.
Values may be sent and summed in bfloat16 or wider, within the bound.
A program may use at most 64 MiB of HBM per device.

v0:
```python
import jax
import jax.numpy as jnp
from jax import lax
from jax.sharding import PartitionSpec as P

RANK = 256


def partner(value, axis, stride):
    mask = 2**stride
    pairs = [(source, source ^ mask) for source in range(lax.axis_size(axis))]
    return lax.ppermute(value, axis, pairs)


def inner_rows(left, right):
    return lax.dot_general(
        left,
        right,
        (((0,), (0,)), ((), ())),
        precision=lax.Precision.HIGHEST,
        preferred_element_type=jnp.float32,
    )


def leaf_total(partial_gram):
    return partial_gram + partner(partial_gram, "row", 0)


def per_device(front_rows, random_columns):
    block_rows = front_rows.shape[0]
    col_count = lax.axis_size("col")
    col_index = lax.axis_index("col")
    row_index = lax.axis_index("row")
    own_rows = block_rows // col_count
    partial_value = jnp.dot(
        front_rows,
        lax.all_gather(random_columns, "row", axis=1, tiled=True).astype(jnp.float32),
        precision=lax.Precision.HIGHEST,
        preferred_element_type=jnp.float32,
    )
    whole = lax.psum(partial_value, "col")
    local_gram = inner_rows(whole[:, :RANK], whole)
    mine = lax.dynamic_slice_in_dim(whole, col_index * own_rows, own_rows, 0)
    gram = leaf_total(local_gram)
    lower = jnp.linalg.cholesky(gram[:, :RANK])
    basis = lax.linalg.triangular_solve(
        lower, mine[:, :RANK], left_side=False, lower=True, transpose_a=True
    )
    coupling = lax.linalg.triangular_solve(lower, gram, left_side=True, lower=True)
    half = RANK // 2
    projected = lax.dynamic_slice_in_dim(coupling, row_index % 2 * half, half, 0)
    return (basis, projected)


def solution(mesh):
    return jax.shard_map(
        per_device,
        mesh=mesh,
        in_specs=(P(("front", "row"), "col"), P(("front", "col"), "row")),
        out_specs=(P(("front", "row", "col"), None), P(("front", "row"), None)),
        check_vma=False,
    )
```

profile of v0, /device:TPU:0, one launch (start us, length us, event | category | flops | bytes accessed | tf_op | source)
XLA Modules:
  0.0 239.0 jit_solution(649683142217514492)
XLA Ops:
  7.2 0.0 all-gather.2.cloned.1.call-start
  7.2 0.7 all-gather.2.cloned.1.call-update
  7.9 0.0 all-reduce.3.cloned.1.call-start
  7.9 74.5 %all-gather.2.cloned.1.call-done = bf16[6144,512]{1,0:T(8,128)(2,1)} async-done(((bf16[6144,128]{1,0:T(8,128)(2,1)}), bf16[6144,512]{1,0:T(8,128)(2,1)}) %all-gather.2.cloned.1.call-update) | async-done | bytes 6291472 | tf_op jit(solution)/shard_map/all_gather | solution.py:37
  82.4 14.8 %fusion.18 = f32[512,512]{1,0:T(8,128)} fusion(f32[512,6144]{1,0:T(8,128)} %param.2, bf16[6144,512]{1,0:T(8,128)(2,1)} %all-gather.2.cloned.1.call-done), kind=kOutput, calls=%fused_computation.41 | convolution fusion | flops 19327352832 | bytes 19922944 | tf_op jit(solution)/shard_map/dot_general | solution.py:35
  97.2 0.0 all-reduce.3.cloned.1.call-update
  97.3 52.1 %all-reduce.3.cloned.1.call-done = f32[512,512]{1,0:T(8,128)} async-done(((f32[512,512]{1,0:T(8,128)}), f32[512,512]{1,0:T(8,128)}) %all-reduce.3.cloned.1.call-update) | async-done | bytes 1048592 | tf_op jit(solution)/shard_map/psum | solution.py:41
  149.3 3.2 %fusion = f32[256,512]{0,1:T(8,128)S(1)} fusion(f32[512,512]{1,0:T(8,128)} %all-reduce.3.cloned.1.call-done), kind=kOutput, calls=%fused_computation.4 | convolution fusion | flops 805306368 | bytes 2097152 | tf_op jit(solution)/shard_map/dot_general | solution.py:16
  152.5 1.5 collective-permute-start
  154.1 12.3 %collective-permute-done = f32[256,512]{0,1:T(8,128)S(1)} collective-permute-done((f32[256,512]{0,1:T(8,128)S(1)}, f32[256,512]{0,1:T(8,128)S(1)}, u32[]{:S(2)}, u32[]{:S(2)}) %collective-permute-start) | collective-permute-done | bytes 524320 | tf_op jit(solution)/shard_map/ppermute | solution.py:12
  166.4 0.1 add.40
  166.5 0.1 copy.6
  166.7 11.7 %cholesky.50 = f32[128,128]{1,0:T(8,128)S(1)} custom-call(f32[128,128]{1,0:T(8,128)S(1)} %cholesky.118), custom_call_target="Cholesky" | custom-call | tf_op jit(solution)/shard_map/jit(cholesky)/cholesky | solution.py:45
  178.4 9.8 %custom-call.16 = f32[1,128,128]{1,2,0:T(8,128)S(1)} custom-call(f32[1,128,128]{2,1,0:T(8,128)S(1)} %get-tuple-element.25), custom_call_target="InvertDiagBlocksLowerTriangular" | custom-call | tf_op jit(solution)/shard_map/jit(cholesky)/cholesky | solution.py:45
  188.3 0.2 constant_dynamic-update-slice_fusion
  188.5 0.3 convolution_subtract_fusion.1
  188.7 11.9 %cholesky.105 = f32[128,128]{1,0:T(8,128)S(1)} custom-call(f32[128,128]{1,0:T(8,128)S(1)} %convolution_subtract_fusion.1), custom_call_target="Cholesky" | custom-call | tf_op jit(solution)/shard_map/jit(cholesky)/cholesky | solution.py:45
  200.6 0.7 compare_reduce_fusion
  202.7 0.1 triangular_solve.73
  202.8 4.1 %while.1 = (s32[]{:T(128)}, f32[256,256]{1,0:T(8,128)S(1)}, s32[2,2]{1,0:T(2,128)S(1)}, f32[2,128,128]{2,1,0:T(8,128)S(1)}, s32[]{:T(128)}) while((s32[]{:T(128)}, f32[256,256]{1,0:T(8,128)S(1)}, s32[2,2]{1,0:T(2,128)S(1)}, f32[2,128,128]{2,1,0:T(8,128)S(1)}, s32[]{:T(128)}) %tuple.28), condition=%wide.while_cond, body=%wide.while_body.sunk | while | flops 2 | bytes 131181 | solution.py:46
  202.8 0.6 fusion.28
  203.4 1.4 bitcast_dynamic-update-slice_fusion.2
  204.9 0.6 fusion.28
  205.5 1.4 bitcast_dynamic-update-slice_fusion.2
  206.9 19.7 %custom-call.17 = f32[2,128,128]{1,2,0:T(8,128)S(1)} custom-call(f32[2,128,128]{2,1,0:T(8,128)S(1)} %get-tuple-element.9), custom_call_target="InvertDiagBlocksLowerTriangular" | custom-call | tf_op jit(solution)/shard_map/triangular_solve | solution.py:46
  226.6 0.4 fusion.4
  227.0 0.6 fusion.13
  227.6 0.4 fusion.3
  228.0 1.1 fusion.9
  229.2 1.1 convolution_subtract_fusion
  230.3 0.3 fusion.12
  230.6 0.8 copy.7
  231.4 0.8 fusion.2
  (12 shorter events, 0.2 us)
Async XLA Ops:
  7.2 75.3 %all-gather.2.cloned.1.call-start = ((), (), s32[]{:S(2)}) async-start(), calls=%async_computation | async-start | bytes 7864320 | tf_op jit(solution)/shard_map/all_gather | solution.py:37
  7.9 141.4 %all-reduce.3.cloned.1.call-start = ((), (), s32[]{:S(2)}) async-start(), calls=%async_computation.1 | async-start | bytes 2097152 | tf_op jit(solution)/shard_map/psum | solution.py:41
  152.5 13.8 %collective-permute-start = (f32[256,512]{0,1:T(8,128)S(1)}, f32[256,512]{0,1:T(8,128)S(1)}, u32[]{:S(2)}, u32[]{:S(2)}) collective-permute-start(f32[256,512]{0,1:T(8,128)S(1)} %fusion), channel_id=1, source_target_pairs={{0,4},{4,0},{8,12},{12,8},{1,5},{5,1},{9,13},{13,9},{2,6},{6,2},{1... | collective-permute-start | bytes 1572872 | tf_op jit(solution)/shard_map/ppermute | solution.py:12
Sparse Core Ops, SparseCore 0:
  9.8 72.6 all-gather.1
  97.4 51.8 all-reduce.2
where the time goes:
time: 239 us
  waiting for transfers between devices  140 us (59%)
  other arithmetic  54.7 us (23%)
  matrix products  22.5 us (9%)
  between operations  15.5 us (6%)
  local copies, waits for them, and re-layouts  5.06 us (2%)
    all_gather x1, waiting for transfers between devices, per_device(): lax.all_gather(random_columns, 'row', axis=1, tiled=True)  74.5 us
    psum x1, waiting for transfers between devices, per_device(): whole = lax.psum(partial_value, 'col')  52.1 us
    another operation x6, other arithmetic, per_device(): lower = jnp.linalg.cholesky(gram[:, :RANK])  34.2 us
    another operation x4, other arithmetic, per_device(): lax.linalg.triangular_solve(lower, mine[:, :RANK], left_side=False, lower...  19.7 us
    dot_general x1, matrix products, per_device(): jnp.dot(front_rows, lax.all_gather(random_columns, 'row', axis=1, tiled=T...  14.8 us
    ppermute x1, waiting for transfers between devices, partner(): return lax.ppermute(value, axis, pairs)  12.3 us
  transfers between devices with their start and end apart: 3, of which 3 were waited for; matrix products, arithmetic and copies ran while one was open for 0% of the time, Pallas kernels for 0%

commit v1 on v0

--- a/solution.py
+++ b/solution.py
@@ -38,7 +38,9 @@
         precision=lax.Precision.HIGHEST,
         preferred_element_type=jnp.float32,
     )
-    whole = lax.psum(partial_value, "col")
+    whole = partial_value
+    for hop in (1, 2):
+        whole = whole + lax.ppermute(whole, "col", [(dev, dev ^ hop) for dev in range(4)])
     local_gram = inner_rows(whole[:, :RANK], whole)
     mine = lax.dynamic_slice_in_dim(whole, col_index * own_rows, own_rows, 0)
     gram = leaf_total(local_gram)

time: 239 us -> 254 us (1.063)
  waiting for transfers between devices: 140 us -> 155 us
  starting transfers between devices: 1.61 us -> 5.58 us
  matrix products: 22.5 us -> 18.6 us
    ppermute x0 -> x2, waiting for transfers between devices: none -> 68.1 us  [per_device(): lax.ppermute(whole, 'col', [(dev, dev ^ hop) for dev in range(4)])]
    psum x1 -> x0, waiting for transfers between devices: 52.1 us -> none  [per_device(): whole = lax.psum(partial_value, 'col')]
    ppermute x0 -> x2, starting transfers between devices: none -> 4.02 us  [per_device(): lax.ppermute(whole, 'col', [(dev, dev ^ hop) for dev in range(4)])]
  transfers between devices with their start and end apart: 3 -> 4, of which waited for: 3 -> 4; matrix products, arithmetic and copies ran while one was open for 0% -> 0% of each run, Pallas kernels for 0% -> 0%
where the time goes in v1:
time: 254 us
  waiting for transfers between devices  155 us (61%)
  other arithmetic  55.1 us (22%)
  matrix products  18.6 us (7%)
  between operations  15.4 us (6%)
  starting transfers between devices  5.58 us (2%)
  local copies, waits for them, and re-layouts  4.78 us (2%)
    all_gather x1, waiting for transfers between devices, per_device(): lax.all_gather(random_columns, 'row', axis=1, tiled=True)  74.6 us
    ppermute x2, waiting for transfers between devices, per_device(): lax.ppermute(whole, 'col', [(dev, dev ^ hop) for dev in range(4)])  68.1 us
    another operation x6, other arithmetic, per_device(): lower = jnp.linalg.cholesky(gram[:, :RANK])  34.1 us
    another operation x4, other arithmetic, per_device(): lax.linalg.triangular_solve(lower, mine[:, :RANK], left_side=False, lower...  19.7 us
    dot_general x1, matrix products, per_device(): jnp.dot(front_rows, lax.all_gather(random_columns, 'row', axis=1, tiled=T...  14 us
    ppermute x1, waiting for transfers between devices, partner(): return lax.ppermute(value, axis, pairs)  11.5 us
  transfers between devices with their start and end apart: 4, of which 4 were waited for; matrix products, arithmetic and copies ran while one was open for 0% of the time, Pallas kernels for 0%

profile of v1, /device:TPU:0, one launch (start us, length us, event | category | flops | bytes accessed | tf_op | source)
XLA Modules:
  0.0 254.3 jit_solution(11963640298133697085)
XLA Ops:
  7.2 0.0 all-gather.2.cloned.1.call-start
  7.2 0.7 all-gather.2.cloned.1.call-update
  7.9 74.6 %all-gather.2.cloned.1.call-done = bf16[6144,512]{1,0:T(8,128)(2,1)} async-done(((bf16[6144,128]{1,0:T(8,128)(2,1)}), bf16[6144,512]{1,0:T(8,128)(2,1)}) %all-gather.2.cloned.1.call-update) | async-done | bytes 6291472 | tf_op jit(solution)/shard_map/all_gather | solution.py:37
  82.4 14.0 %fusion.19 = f32[512,512]{1,0:T(8,128)S(1)} fusion(f32[512,6144]{1,0:T(8,128)} %param.2, bf16[6144,512]{1,0:T(8,128)(2,1)} %all-gather.2.cloned.1.call-done), kind=kOutput, calls=%fused_computation.42 | convolution fusion | flops 19327352832 | bytes 19922944 | tf_op jit(solution)/shard_map/dot_general | solution.py:35
  96.4 1.6 collective-permute-start
  98.0 23.2 %collective-permute-done = f32[512,512]{1,0:T(8,128)S(1)} collective-permute-done((f32[512,512]{1,0:T(8,128)S(1)}, f32[512,512]{1,0:T(8,128)S(1)}, u32[]{:S(2)}, u32[]{:S(2)}) %collective-permute-start) | collective-permute-done | bytes 1048608 | tf_op jit(solution)/shard_map/ppermute | solution.py:43
  121.2 0.2 add.43
  121.5 2.5 collective-permute-start.1
  123.9 44.8 %collective-permute-done.1 = f32[512,512]{1,0:T(8,128)S(1)} collective-permute-done((f32[512,512]{1,0:T(8,128)S(1)}, f32[512,512]{1,0:T(8,128)S(1)}, u32[]{:S(2)}, u32[]{:S(2)}) %collective-permute-start.1) | collective-permute-done | bytes 1048608 | tf_op jit(solution)/shard_map/ppermute | solution.py:43
  168.8 0.2 add.44
  169.0 1.8 fusion
  170.8 1.5 collective-permute-start.2
  172.3 11.5 %collective-permute-done.2 = f32[256,512]{0,1:T(8,128)S(1)} collective-permute-done((f32[256,512]{0,1:T(8,128)S(1)}, f32[256,512]{0,1:T(8,128)S(1)}, u32[]{:S(2)}, u32[]{:S(2)}) %collective-permute-start.2) | collective-permute-done | bytes 524320 | tf_op jit(solution)/shard_map/ppermute | solution.py:12
  183.8 0.1 add.46
  183.9 0.1 copy.6
  184.1 11.7 %cholesky.50 = f32[128,128]{1,0:T(8,128)S(1)} custom-call(f32[128,128]{1,0:T(8,128)S(1)} %cholesky.118), custom_call_target="Cholesky" | custom-call | tf_op jit(solution)/shard_map/jit(cholesky)/cholesky | solution.py:47
  195.8 9.8 %custom-call.16 = f32[1,128,128]{1,2,0:T(8,128)S(1)} custom-call(f32[1,128,128]{2,1,0:T(8,128)S(1)} %get-tuple-element.25), custom_call_target="InvertDiagBlocksLowerTriangular" | custom-call | tf_op jit(solution)/shard_map/jit(cholesky)/cholesky | solution.py:47
  205.7 0.2 constant_dynamic-update-slice_fusion
  205.9 0.3 convolution_subtract_fusion
  206.2 11.9 %cholesky.105 = f32[128,128]{1,0:T(8,128)S(1)} custom-call(f32[128,128]{1,0:T(8,128)S(1)} %convolution_subtract_fusion), custom_call_target="Cholesky" | custom-call | tf_op jit(solution)/shard_map/jit(cholesky)/cholesky | solution.py:47
  218.1 0.6 compare_reduce_fusion
  220.0 0.1 triangular_solve.73
  220.1 3.8 %while.1 = (s32[]{:T(128)}, f32[256,256]{1,0:T(8,128)S(1)}, s32[2,2]{1,0:T(2,128)S(1)}, f32[2,128,128]{2,1,0:T(8,128)S(1)}, s32[]{:T(128)}) while((s32[]{:T(128)}, f32[256,256]{1,0:T(8,128)S(1)}, s32[2,2]{1,0:T(2,128)S(1)}, f32[2,128,128]{2,1,0:T(8,128)S(1)}, s32[]{:T(128)}) %tuple.28), condition=%wide.while_cond, body=%wide.while_body.sunk | while | flops 2 | bytes 131181 | solution.py:48
  220.1 0.6 fusion.28
  220.7 1.3 bitcast_dynamic-update-slice_fusion.2
  222.0 0.6 fusion.28
  222.6 1.3 bitcast_dynamic-update-slice_fusion.2
  223.9 19.7 %custom-call.17 = f32[2,128,128]{1,2,0:T(8,128)S(1)} custom-call(f32[2,128,128]{2,1,0:T(8,128)S(1)} %get-tuple-element.9), custom_call_target="InvertDiagBlocksLowerTriangular" | custom-call | tf_op jit(solution)/shard_map/triangular_solve | solution.py:48
  243.6 0.4 fusion.4
  244.0 0.6 fusion.13
  244.6 0.4 fusion.3
  245.0 0.3 fusion.10
  245.3 0.3 fusion.15
  245.6 0.3 fusion.7
  246.0 0.8 copy.7
  246.7 0.8 fusion.2
  (12 shorter events, 0.2 us)
Async XLA Ops:
  7.2 75.3 %all-gather.2.cloned.1.call-start = ((), (), s32[]{:S(2)}) async-start(), calls=%async_computation | async-start | bytes 7864320 | tf_op jit(solution)/shard_map/all_gather | solution.py:37
  96.4 24.8 %collective-permute-start = (f32[512,512]{1,0:T(8,128)S(1)}, f32[512,512]{1,0:T(8,128)S(1)}, u32[]{:S(2)}, u32[]{:S(2)}) collective-permute-start(f32[512,512]{1,0:T(8,128)S(1)} %fusion.19), channel_id=1, source_target_pairs={{0,1},{1,0},{2,3},{3,2},{4,5},{5,4},{6,7},{7,6},{8,9},{9,8},{10,11... | collective-permute-start | bytes 3145736 | tf_op jit(solution)/shard_map/ppermute | solution.py:43
  121.5 47.3 %collective-permute-start.1 = (f32[512,512]{1,0:T(8,128)S(1)}, f32[512,512]{1,0:T(8,128)S(1)}, u32[]{:S(2)}, u32[]{:S(2)}) collective-permute-start(f32[512,512]{1,0:T(8,128)S(1)} %add.43), channel_id=1, source_target_pairs={{0,2},{1,3},{2,0},{3,1},{4,6},{5,7},{6,4},{7,5},{8,10},{9,11},{10,... | collective-permute-start | bytes 3145736 | tf_op jit(solution)/shard_map/ppermute | solution.py:43
  170.8 13.0 %collective-permute-start.2 = (f32[256,512]{0,1:T(8,128)S(1)}, f32[256,512]{0,1:T(8,128)S(1)}, u32[]{:S(2)}, u32[]{:S(2)}) collective-permute-start(f32[256,512]{0,1:T(8,128)S(1)} %fusion), channel_id=1, source_target_pairs={{0,4},{4,0},{8,12},{12,8},{1,5},{5,1},{9,13},{13,9},{2,6},{6,2},{1... | collective-permute-start | bytes 1572872 | tf_op jit(solution)/shard_map/ppermute | solution.py:12
Sparse Core Ops, SparseCore 0:
  9.8 72.6 all-gather.1
